TPU v7x, 32 devices: a whole 2x2x4 slice. The times are simulated.
32 devices in a mesh: groups: 1, slab: 8 (over z, y), coil: 2 (over x), row: 2 (over core).
Axes of the slice: x: 2, y: 2, z: 4, core: 2. Of those that a mesh axis runs over, the one named last changes fastest.
Arguments:
- image: float32 [2, 128, 256, 128], P('groups', None, ('slab', 'row')), may hold values from -6 to 6
- sens: bfloat16 [2, 16, 128, 256, 128], P('groups', 'coil', None, ('slab', 'row')), may hold values from -1.5 to 1.5
- measured: bfloat16 [2, 16, 128, 256, 128], P('groups', 'coil', ('slab', 'row')), may hold values from -3 to 3
- mask: int32 [128, 256], P(('slab', 'row')), may hold values from 0 to 1, as said below
- thresholds: float32 [2, 7], replicated, may hold values from 0.1 to 1.5
Outputs:
- image_next: float32 [2, 128, 256, 128], P('groups', None, ('slab', 'row'))
Inputs may be any that keep to these rules, and one draw needn't show every extreme that they name: `mask`: A calibration block of the 8 central phase-encode lines (ky from 60 to 67) is sampled at every kz; outside it each (ky, kz) is sampled independently at random.
All inputs are finite; a program needn't handle non-finite values.
Results may differ from a plain program's by a relative error of at most 0.013.
Values may be sent and summed in bfloat16 or wider, within the bound.
A program may use at most 128 MiB of HBM per device.

v0:
```python
import math

import jax
import jax.numpy as jnp
from jax import lax
from jax.sharding import PartitionSpec as P

half_root = 0.7071067811865476
quarter_root = 0.3535533905932738
step_size = 0.5


def passed_along(block, axis, distance):
    devices = range(lax.axis_size(axis))
    route = [((i - distance) % len(devices), i) for i in devices]
    return lax.ppermute(block, axis, route)


def fourier_table(length, sign):
    index = jnp.arange(length, dtype=jnp.int32)
    phase = index[:, None] * index[None, :] % length
    theta = phase.astype(jnp.float32) * jnp.float32(2.0 * math.pi / length)
    scale = jnp.float32(1.0 / math.sqrt(length))
    real = jnp.cos(theta) * scale
    imaginary = jnp.sin(theta) * (sign * scale)
    upper = jnp.stack([real, -imaginary])
    lower = jnp.stack([imaginary, real])
    return jnp.stack([upper, lower]).astype(jnp.bfloat16)


def contract(form, values, table):
    return jnp.einsum(form, values, table, preferred_element_type=jnp.float32)


def complex_product(left, right):
    return jnp.stack(
        [left[0] * right[0] - left[1] * right[1], left[0] * right[1] + left[1] * right[0]]
    )


def roll_after(values, along, offset):
    return jnp.roll(values, -offset, axis=along)


def roll_before(values, along, offset):
    return jnp.roll(values, offset, axis=along)


def plane_after(values, along, offset):
    border = lax.slice_in_dim(values, 0, offset, axis=along)
    fetched = passed_along(border.astype(jnp.bfloat16), ("slab", "row"), -1).astype(border.dtype)
    remain = lax.slice_in_dim(values, offset, values.shape[along], axis=along)
    return jnp.concatenate([remain, fetched], axis=along)


def plane_before(values, along, offset):
    extent = values.shape[along]
    border = lax.slice_in_dim(values, extent - offset, extent, axis=along)
    fetched = passed_along(border.astype(jnp.bfloat16), ("slab", "row"), 1).astype(border.dtype)
    remain = lax.slice_in_dim(values, 0, extent - offset, axis=along)
    return jnp.concatenate([fetched, remain], axis=along)


def split_bands(bands, along, offset, after):
    moved = after(bands, along, offset)
    return jnp.concatenate([(bands + moved) * half_root, (bands - moved) * half_root], axis=0)


def merge_bands(bands, along, offset, before):
    half = bands.shape[0] // 2
    lower = bands[:half]
    upper = bands[half:]
    return (lower + upper + before(lower - upper, along, offset)) * quarter_root


def shrink_detail(detail, limit):
    magnitude = jnp.sqrt(detail[:, 0] * detail[:, 0] + detail[:, 1] * detail[:, 1])
    limit = limit.reshape((-1, 1, 1, 1))
    factor = jnp.maximum(magnitude - limit, 0.0) / jnp.maximum(magnitude, limit)
    return detail * factor[:, None]


def wavelet_shrink(descent, thresholds, moves):
    coarse = descent[None]
    details = []
    for level in range(thresholds.shape[0]):
        offset = 2**level
        bands = coarse
        for along, after, before in moves:
            bands = split_bands(bands, along, offset, after)
        coarse = bands[:1]
        details.append(shrink_detail(bands[1:], thresholds[level]))
    for level in reversed(range(thresholds.shape[0])):
        offset = 2**level
        bands = jnp.concatenate([coarse, details[level]], axis=0)
        for along, after, before in reversed(moves):
            bands = merge_bands(bands, along, offset, before)
        coarse = bands
    return coarse[0]


def local(image, sens, measured, mask, thresholds):
    readout_cells = image.shape[3]
    phase_cells = image.shape[1]
    depth_cells = measured.shape[3]
    table_readout = fourier_table(readout_cells, -1.0)
    table_phase = fourier_table(phase_cells, -1.0)
    table_depth = fourier_table(depth_cells, -1.0)
    inverse_readout = fourier_table(readout_cells, 1.0)
    inverse_phase = fourier_table(phase_cells, 1.0)
    inverse_depth = fourier_table(depth_cells, 1.0)
    sens_wide = sens.astype(jnp.float32)
    coil_image = complex_product(sens_wide, image[:, None]).astype(jnp.bfloat16)
    readout_done = contract("tcyzj,stjk->scyzk", coil_image, table_readout).astype(jnp.bfloat16)
    phase_done = contract("tcjzx,stjk->sckzx", readout_done, table_phase).astype(jnp.bfloat16)
    spread = lax.all_to_all(phase_done, ("slab", "row"), split_axis=2, concat_axis=3, tiled=True)
    spectrum = contract("tcyjx,stjk->scykx", spread, table_depth)
    sampled = mask.astype(jnp.float32)[None, None, :, :, None]
    residual = (sampled * (spectrum - measured.astype(jnp.float32))).astype(jnp.bfloat16)
    depth_back = contract("tcyjx,stjk->scykx", residual, inverse_depth).astype(jnp.bfloat16)
    gathered = lax.all_to_all(depth_back, ("slab", "row"), split_axis=3, concat_axis=2, tiled=True)
    phase_back = contract("tcjzx,stjk->sckzx", gathered, inverse_phase).astype(jnp.bfloat16)
    readout_back = contract("tcyzj,stjk->scyzk", phase_back, inverse_readout)
    partial_value = jnp.stack(
        [
            jnp.sum(sens_wide[0] * readout_back[0] + sens_wide[1] * readout_back[1], axis=0),
            jnp.sum(sens_wide[0] * readout_back[1] - sens_wide[1] * readout_back[0], axis=0),
        ]
    )
    gradient = lax.psum(partial_value.astype(jnp.bfloat16), "coil").astype(jnp.float32)
    descent = image - step_size * gradient
    moves = [
        (4, roll_after, roll_before),
        (2, roll_after, roll_before),
        (3, plane_after, plane_before),
    ]
    return wavelet_shrink(descent, thresholds, moves)


def solution(mesh):
    return jax.shard_map(
        local,
        mesh=mesh,
        in_specs=(
            P("groups", None, ("slab", "row"), None),
            P("groups", "coil", None, ("slab", "row"), None),
            P("groups", "coil", ("slab", "row"), None, None),
            P(("slab", "row"), None),
            P(),
        ),
        out_specs=P("groups", None, ("slab", "row"), None),
        check_vma=False,
    )
```

profile of v0, /device:TPU:0, one launch (start us, length us, event | category | flops | bytes accessed | tf_op | source)
XLA Modules:
  0.0 727.1 jit_solution(10082498368846165496)
XLA Ops:
  7.4 11.7 %copy_convert_fusion = f32[2,8,128,16,128]{4,2,0,3,1:T(8,128)} fusion(bf16[2,8,128,16,128]{4,3,2,1,0:T(8,128)(2,1)} %param.6), kind=kLoop, calls=%fused_computation.53 | loop fusion | flops 4194304 | bytes 25165824 | tf_op jit(solution)/shard_map/convert_element_type | solution.py:112
  20.0 9.6 %subtract_convert_fusion = (bf16[1,8,128,16,128]{4,2,0,3,1:T(8,128)(2,1)}, bf16[1,8,128,16,128]{4,2,0,3,1:T(8,128)(2,1)}) fusion(f32[2,8,128,16,128]{4,2,0,3,1:T(8,128)} %copy_convert_fusion, f32[128,16,128]{2,0,1:T(8,128)S(1)} %copy.36, f32[128,16,128]{2,0,1:T(8,128)S(1)} %copy.35), kind=kLoop, calls=%fused_computation.61 | loop fusion | flops 16777216 | bytes 27262976 | tf_op jit(solution)/shard_map/convert.8
  29.5 9.1 %fusion.6 = bf16[2,8,128,16,128]{4,2,3,1,0:T(8,128)(2,1)} fusion(bf16[1,8,128,16,128]{4,2,0,3,1:T(8,128)(2,1)} %get-tuple-element.8, bf16[1,8,128,16,128]{4,2,0,3,1:T(8,128)(2,1)} %get-tuple-element.7, bf16[1,2,128,128]{2,3,1,0:T(8,128)(2,1)S(1)} %get-tuple-element.28, bf16[1,2,128,128]{2,3,1,0:T(8,128)(2,1)S(1)} %get-tuple-element.29), kind=kOutput, calls=%fused_computation.30 | convolution fusion | flops 4320657408 | bytes 16908288 | tf_op jit(solution)/shard_map/tcjzx,stjk->sckzx/dot_general | solution.py:32
  38.6 12.0 %copy.38 = bf16[2,8,128,16,128]{4,3,1,0,2:T(8,128)(2,1)} copy(bf16[2,8,128,16,128]{4,2,3,1,0:T(8,128)(2,1)} %fusion.6) | data formatting | bytes 16777216 | tf_op jit(solution)/shard_map/convert_element_type | solution.py:115
  50.6 7.6 %all-to-all-start = ((bf16[2,8,128,16,128]{4,3,1,0,2:T(8,128)(2,1)}), bf16[2,8,128,16,128]{4,3,1,0,2:T(8,128)(2,1)}, u32[]{:S(2)}, u32[]{:S(2)}) async-start(bf16[2,8,128,16,128]{4,3,1,0,2:T(8,128)(2,1)} %copy.38), calls=%async_computation | async-start | bytes 16777216 | tf_op jit(solution)/shard_map/all_to_all | solution.py:116
  61.7 147.1 %all-to-all-done = bf16[2,8,128,16,128]{4,3,1,0,2:T(8,128)(2,1)} async-done(((bf16[2,8,128,16,128]{4,3,1,0,2:T(8,128)(2,1)}), bf16[2,8,128,16,128]{4,3,1,0,2:T(8,128)(2,1)}, u32[]{:S(2)}, u32[]{:S(2)}) %all-to-all-start) | async-done | bytes 8388640 | tf_op jit(solution)/shard_map/all_to_all | solution.py:116
  208.8 9.1 %copy.40 = bf16[2,8,8,16,16,128]{5,4,3,2,1,0:T(8,128)(2,1)} copy(bf16[2,8,8,16,16,128]{5,4,1,0,2,3:T(8,128)(2,1)} %bitcast.31) | data formatting | bytes 16777216 | tf_op jit(solution)/shard_map/all_to_all | solution.py:116
  218.0 9.5 %fusion.1 = bf16[2,8,8,256,128]{4,3,2,1,0:T(8,128)(2,1)S(1)} fusion(bf16[2,8,8,256,128]{4,3,2,1,0:T(8,128)(2,1)} %param.7, f32[8,256]{1,0:T(8,128)S(1)} %convert_element_type.150, bf16[2,8,8,256,128]{4,3,2,1,0:T(8,128)(2,1)} %bitcast.172, bf16[1,2,256,256]{2,3,1,0:T(8,128)(2,1)S(1)} %get-tuple-element.24, bf16[1,2,256,256]{2,3,1,0:T(8,128)(2,1)S(1)} %get-tuple-element.25), kind=kOutput, calls=%fused_computation.10 | convolution fusion | flops 4312793088 | bytes 25698304 | tf_op jit(solution)/shard_map/tcyjx,stjk->scykx/dot_general | solution.py:32
  234.2 12.1 %copy.43 = bf16[2,8,8,256,128]{4,2,1,0,3:T(8,128)(2,1)} copy(bf16[2,8,8,256,128]{4,3,2,1,0:T(8,128)(2,1)} %fusion.7) | data formatting | bytes 16777216 | tf_op jit(solution)/shard_map/convert_element_type | solution.py:120
  246.3 219.0 %all_to_all.36 = bf16[2,8,8,256,128]{4,2,1,0,3:T(8,128)(2,1)} all-to-all(bf16[2,8,8,256,128]{4,2,1,0,3:T(8,128)(2,1)} %copy.43), channel_id=1, replica_groups=mesh['groups'=1,'slab'=8,'coil'=2,'row'=2] {'slab','row'}, dimensions={3} | all-to-all | bytes 16777216 | tf_op jit(solution)/shard_map/all_to_all | solution.py:121
  465.3 16.3 %copy.45 = bf16[2,8,16,8,16,128]{5,4,3,2,1,0:T(8,128)(2,1)} copy(bf16[2,8,16,8,16,128]{5,3,1,0,4,2:T(8,128)(2,1)} %bitcast.169) | data formatting | bytes 16777216 | tf_op jit(solution)/shard_map/all_to_all | solution.py:121
  481.6 12.3 %convolution_bitcast_fusion = f32[2,8,128,16,128]{4,2,0,3,1:T(8,128)} fusion(bf16[2,8,128,16,128,1]{4,3,2,1,0,5:T(8,128)(2,1)} %bitcast.168, bf16[1,2,128,128]{2,3,1,0:T(8,128)(2,1)S(1)} %get-tuple-element.30, bf16[1,2,128,128]{2,3,1,0:T(8,128)(2,1)S(1)} %get-tuple-element.27), kind=kOutput, calls=%fused_computation.29 | convolution fusion | flops 4299685888 | bytes 25296896 | tf_op jit(solution)/shard_map/tcyzj,stjk->scyzk/dot_general | solution.py:32
  493.9 13.1 %add_reduce_fusion = (bf16[128,16,128]{2,0,1:T(8,128)(2,1)S(1)}, bf16[128,16,128]{2,0,1:T(8,128)(2,1)S(1)}) fusion(f32[2,8,128,16,128]{4,2,0,3,1:T(8,128)} %convolution_bitcast_fusion, f32[2,8,128,16,128]{4,2,0,3,1:T(8,128)} %copy_convert_fusion), kind=kLoop, calls=%fused_computation.59 | loop fusion | flops 16252928 | bytes 34603008 | tf_op jit(solution)/shard_map/reduce_sum | solution.py:126
  510.7 39.3 %all-reduce.2.cloned.1.call-done = bf16[2,128,16,128]{1,3,2,0:T(8,128)(2,1)} async-done(((bf16[2,128,16,128]{1,3,2,0:T(8,128)(2,1)}), bf16[2,128,16,128]{1,3,2,0:T(8,128)(2,1)}) %all-reduce.2.cloned.1.call-update) | async-done | bytes 1048592 | tf_op jit(solution)/shard_map/psum | solution.py:130
  563.7 6.8 subtract_multiply_fusion
  595.9 8.9 %subtract_multiply_fusion.1 = (f32[4,2,128,16,128]{2,4,3,1,0:T(8,128)}, f32[4,2,128,16,128]{2,4,3,1,0:T(8,128)S(1)}) fusion(f32[4,2,128,2,128]{2,4,3,1,0:T(8,128)S(1)} %convert_element_type.163, f32[4,2,128,14,128]{2,4,3,1,0:T(8,128)} %fusion.23, f32[2,2,128,16,128]{2,4,3,1,0:T(8,128)} %copy-done.4, f32[2,2,128,16,128]{2,4,3,1,0:T(8,128)} %copy-done.5), kind=kLoop, calls=%fused_computation.55 | loop fusion | flops 12582912 | bytes 33554432 | tf_op jit(solution)/shard_map/mul | solution.py:66
  608.0 7.7 %divide_bitcast_fusion.1 = f32[7,128,16,128]{1,3,2,0:T(8,128)} fusion(f32[4,2,128,16,128]{2,4,3,1,0:T(8,128)} %get-tuple-element.9, f32[4,2,128,16,128]{2,4,3,1,0:T(8,128)S(1)} %get-tuple-element.10, f32[7]{0:T(128)S(1)} %get-tuple-element.31), kind=kLoop, calls=%fused_computation.79 | loop fusion | flops 16515072 | bytes 24117276 | tf_op jit(solution)/shard_map/mul | solution.py:80
  615.8 8.2 %fusion.5 = f32[7,2,128,16,128]{2,4,3,1,0:T(8,128)S(1)} fusion(f32[4,2,128,16,128]{2,4,3,1,0:T(8,128)} %copy-done.1, f32[4,2,128,16,128]{2,4,3,1,0:T(8,128)} %get-tuple-element.9, f32[7,128,16,128]{1,3,2,0:T(8,128)} %divide_bitcast_fusion.1), kind=kLoop, calls=%fused_computation.18 | loop fusion | flops 7340032 | bytes 38797312 | tf_op jit(solution)/shard_map/mul | solution.py:80
  629.5 11.6 %fusion.3 = f32[7,2,128,16,128]{2,4,3,1,0:T(8,128)} fusion(f32[4,2,128,16,128]{2,4,3,1,0:T(8,128)S(1)} %bitcast.165, f32[4,2,128,16,128]{2,4,3,1,0:T(8,128)} %copy-done.3, f32[7,128,16,128]{1,3,2,0:T(8,128)} %divide_bitcast_fusion), kind=kLoop, calls=%fused_computation.16 | loop fusion | flops 7340032 | bytes 38797312 | tf_op jit(solution)/shard_map/mul | solution.py:80
  641.1 6.9 slice.282
  648.1 6.9 fusion.10
  662.5 9.9 %fusion.44 = f32[2,2,128,16,128]{2,4,3,1,0:T(8,128)} fusion(f32[2,2,126,16,128]{2,4,3,1,0:T(8,128)} %bitcast.166, f32[2,2,2,16,128]{2,4,3,1,0:T(8,128)} %slice.285, f32[4,2,128,16,128]{2,4,3,1,0:T(8,128)} %fusion.10), kind=kLoop, calls=%fused_computation.97 | loop fusion | flops 4194304 | bytes 16777216 | tf_op jit(solution)/shard_map/mul | solution.py:73
  683.3 7.3 %slice.297 = f32[4,2,128,15,128]{2,4,3,1,0:T(8,128)} slice(f32[4,2,128,16,128]{2,4,3,1,0:T(8,128)} %copy-done.10), slice={[0:4], [0:2], [0:128], [0:15], [0:128]} | slice | bytes 15728640 | tf_op jit(solution)/shard_map/slice | solution.py:60
  691.8 7.1 fusion.11
  (111 shorter events, 103.6 us)
Async XLA Ops:
  7.4 11.7 %copy-start.11 = (f32[2,128,16,128]{3,2,1,0:T(8,128)S(1)}, f32[2,128,16,128]{3,2,1,0:T(8,128)}, u32[]{:S(2)}) copy-start(f32[2,128,16,128]{3,2,1,0:T(8,128)} %param.5) | copy-start | bytes 6291460
  50.6 7.7 %copy-start.13 = (s32[8,256]{1,0:T(8,128)S(1)}, s32[8,256]{1,0:T(8,128)}, u32[]{:S(2)}) copy-start(s32[8,256]{1,0:T(8,128)} %param.8) | copy-start | bytes 24580
  50.6 158.2 %all-to-all-start = ((bf16[2,8,128,16,128]{4,3,1,0,2:T(8,128)(2,1)}), bf16[2,8,128,16,128]{4,3,1,0,2:T(8,128)(2,1)}, u32[]{:S(2)}, u32[]{:S(2)}) async-start(bf16[2,8,128,16,128]{4,3,1,0,2:T(8,128)(2,1)} %copy.38), calls=%async_computation | async-start | bytes 16777216 | tf_op jit(solution)/shard_map/all_to_all | solution.py:116
  58.2 491.7 %all-reduce.2.cloned.1.call-start = ((), (), s32[]{:S(2)}) async-start(), calls=%async_computation.2 | async-start | bytes 2097152 | tf_op jit(solution)/shard_map/psum | solution.py:130
  507.0 3.7 copy-start.14
  556.1 7.4 %copy-start.6 = (f32[2,2,128,16,128]{2,4,3,1,0:T(8,128)}, f32[2,2,128,16,128]{2,4,3,1,0:T(8,128)S(1)}, u32[]{:S(2)}) copy-start(f32[2,2,128,16,128]{2,4,3,1,0:T(8,128)S(1)} %get-tuple-element.15) | copy-start | bytes 12582916
  556.1 7.4 %copy-start.7 = (f32[2,2,128,16,128]{2,4,3,1,0:T(8,128)}, f32[2,2,128,16,128]{2,4,3,1,0:T(8,128)S(1)}, u32[]{:S(2)}) copy-start(f32[2,2,128,16,128]{2,4,3,1,0:T(8,128)S(1)} %get-tuple-element.16) | copy-start | bytes 12582916
  556.2 7.5 %collective-permute-start = (bf16[4,2,128,1,128]{2,4,3,1,0:T(8,128)(2,1)S(1)}, bf16[4,2,128,1,128]{2,4,3,1,0:T(8,128)(2,1)S(1)}, u32[]{:S(2)}, u32[]{:S(2)}) collective-permute-start(bf16[4,2,128,1,128]{2,4,3,1,0:T(8,128)(2,1)S(1)} %fusion.61), channel_id=1, source_target_pairs={{1,0},{4,1},{5,4},{8,5},{9,8},{12,9},{13,12},{16,13},{17,16},{20,1... | collective-permute-start | bytes 786440 | tf_op jit(solution)/shard_map/ppermute | solution.py:16
  570.5 16.8 %copy-start = (f32[4,2,128,16,128]{2,4,3,1,0:T(8,128)}, f32[4,2,128,16,128]{2,4,3,1,0:T(8,128)S(1)}, u32[]{:S(2)}) copy-start(f32[4,2,128,16,128]{2,4,3,1,0:T(8,128)S(1)} %get-tuple-element.12) | copy-start | bytes 25165828
  570.5 16.8 %copy-start.3 = (f32[4,2,128,16,128]{2,4,3,1,0:T(8,128)}, f32[4,2,128,16,128]{2,4,3,1,0:T(8,128)S(1)}, u32[]{:S(2)}) copy-start(f32[4,2,128,16,128]{2,4,3,1,0:T(8,128)S(1)} %get-tuple-element.11) | copy-start | bytes 25165828
  582.5 10.1 %copy-start.4 = (f32[2,2,128,16,128]{2,4,3,1,0:T(8,128)}, f32[2,2,128,16,128]{2,4,3,1,0:T(8,128)S(1)}, u32[]{:S(2)}) copy-start(f32[2,2,128,16,128]{2,4,3,1,0:T(8,128)S(1)} %get-tuple-element.13) | copy-start | bytes 12582916
  582.5 10.1 %copy-start.5 = (f32[2,2,128,16,128]{2,4,3,1,0:T(8,128)}, f32[2,2,128,16,128]{2,4,3,1,0:T(8,128)S(1)}, u32[]{:S(2)}) copy-start(f32[2,2,128,16,128]{2,4,3,1,0:T(8,128)S(1)} %get-tuple-element.14) | copy-start | bytes 12582916
  582.6 13.2 %collective-permute-start.1 = (bf16[4,2,128,2,128]{2,4,3,1,0:T(8,128)(2,1)S(1)}, bf16[4,2,128,2,128]{2,4,3,1,0:T(8,128)(2,1)S(1)}, u32[]{:S(2)}, u32[]{:S(2)}) collective-permute-start(bf16[4,2,128,2,128]{2,4,3,1,0:T(8,128)(2,1)S(1)} %fusion.54), channel_id=1, source_target_pairs={{1,0},{4,1},{5,4},{8,5},{9,8},{12,9},{13,12},{16,13},{17,16},{20,1... | collective-permute-start | bytes 1572872 | tf_op jit(solution)/shard_map/ppermute | solution.py:16
  608.0 21.4 %slice-start.4 = ((s8[8388608]{0:T(1024)(128)(4,1)}), s8[4194304]{0:T(1024)(128)(4,1)S(1)}, s32[]{:S(2)}) async-start(s8[8388608]{0:T(1024)(128)(4,1)} %bitcast.164), calls=%async_computation.7 | async-start | bytes 8388608
  615.8 13.6 %slice-start.5 = ((s8[8388608]{0:T(1024)(128)(4,1)}), s8[4194304]{0:T(1024)(128)(4,1)S(1)}, s32[]{:S(2)}) async-start(s8[8388608]{0:T(1024)(128)(4,1)} %bitcast.164), calls=%async_computation.8 | async-start | bytes 8388608
  629.4 18.7 %collective-permute-start.2 = (bf16[4,2,128,2,128]{2,4,3,1,0:T(8,128)(2,1)S(1)}, bf16[4,2,128,2,128]{2,4,3,1,0:T(8,128)(2,1)S(1)}, u32[]{:S(2)}, u32[]{:S(2)}) collective-permute-start(bf16[4,2,128,2,128]{2,4,3,1,0:T(8,128)(2,1)S(1)} %slice.450), channel_id=1, source_target_pairs={{29,0},{0,1},{1,4},{4,5},{5,8},{8,9},{9,12},{12,13},{13,16},{16,17... | collective-permute-start | bytes 1572872 | tf_op jit(solution)/shard_map/ppermute | solution.py:16
  662.5 15.5 %slice-start = ((s8[14680064]{0:T(1024)(128)(4,1)}), s8[4194304]{0:T(1024)(128)(4,1)S(1)}, s32[]{:S(2)}) async-start(s8[14680064]{0:T(1024)(128)(4,1)} %bitcast.162), calls=%async_computation.3 | async-start | bytes 8388608
  662.5 15.5 %slice-start.1 = ((s8[14680064]{0:T(1024)(128)(4,1)}), s8[4194304]{0:T(1024)(128)(4,1)S(1)}, s32[]{:S(2)}) async-start(s8[14680064]{0:T(1024)(128)(4,1)} %bitcast.162), calls=%async_computation.4 | async-start | bytes 8388608
  662.5 15.6 %slice-start.2 = ((s8[14680064]{0:T(1024)(128)(4,1)}), s8[2097152]{0:T(1024)(128)(4,1)S(1)}, s32[]{:S(2)}) async-start(s8[14680064]{0:T(1024)(128)(4,1)} %bitcast.162), calls=%async_computation.5 | async-start | bytes 4194304
  672.4 5.6 slice-start.3
  679.9 3.3 copy-start.10
  683.2 8.5 %collective-permute-start.3 = (bf16[4,2,128,1,128]{2,4,3,1,0:T(8,128)(2,1)S(1)}, bf16[4,2,128,1,128]{2,4,3,1,0:T(8,128)(2,1)S(1)}, u32[]{:S(2)}, u32[]{:S(2)}) collective-permute-start(bf16[4,2,128,1,128]{2,4,3,1,0:T(8,128)(2,1)S(1)} %slice.451), channel_id=1, source_target_pairs={{29,0},{0,1},{1,4},{4,5},{5,8},{8,9},{9,12},{12,13},{13,16},{16,17... | collective-permute-start | bytes 786440 | tf_op jit(solution)/shard_map/ppermute | solution.py:16
  703.2 4.9 copy-start.2
  713.7 3.4 copy-start.9
  (3 other events, 8.3 us)
Sparse Core Ops, SparseCore 0:
  508.8 41.1 all-reduce.1
where the time goes:
time: 731 us; the launch traced here: 727 us
  blocking collectives  219 us (30%)
  waiting for transfers between devices  188 us (26%)
  other arithmetic  166 us (23%)
  local copies, waits for them, and re-layouts  86.6 us (12%)
  matrix products  37.6 us (5%)
  starting transfers between devices  16 us (2%)
  between operations  14.1 us (2%)
    all_to_all x1, blocking collectives, local(): lax.all_to_all(depth_back, ('slab', 'row'), split_axis=3, concat_axis=2,...  219 us
    all_to_all x1, waiting for transfers between devices, local(): lax.all_to_all(phase_done, ('slab', 'row'), split_axis=2, concat_axis=3,...  147 us
    psum x1, waiting for transfers between devices, local(): lax.psum(partial_value.astype(jnp.bfloat16), 'coil').astype(jnp.float32)  39.3 us
    dot_general x4, matrix products, contract(): return jnp.einsum(form, values, table, preferred_element_type=jnp.float32)  37.6 us
    mul x4, other arithmetic, shrink_detail(): return detail * factor[:, None]  32.9 us
    mul x5, other arithmetic, merge_bands(): return (lower + upper + before(lower - upper, along, offset)) * quarter_root  32.5 us
    mul x3, other arithmetic, split_bands(): (bands - moved) * half_root  19.9 us
    sub x6, other arithmetic, merge_bands(): return (lower + upper + before(lower - upper, along, offset)) * quarter_root  19.6 us
  transfers between devices with their start and end apart: 6, of which 4 were waited for; matrix products, arithmetic and copies ran while one was open for 6% of the time, Pallas kernels for 0%

commit v1 on v0

v1 whole, which is shorter than its diff:
```python
import functools
import math

import jax
import jax.numpy as jnp
from jax import lax
from jax.experimental import pallas as pl
from jax.experimental.pallas import tpu as pltpu
from jax.sharding import PartitionSpec as P

half_root = 0.7071067811865476
quarter_root = 0.3535533905932738
step_size = 0.5
CHUNKS = 2


def passed_along(block, axis, distance):
    devices = range(lax.axis_size(axis))
    route = [((i - distance) % len(devices), i) for i in devices]
    return lax.ppermute(block, axis, route)


def fourier_table(length, sign):
    index = jnp.arange(length, dtype=jnp.int32)
    phase = index[:, None] * index[None, :] % length
    theta = phase.astype(jnp.float32) * jnp.float32(2.0 * math.pi / length)
    scale = jnp.float32(1.0 / math.sqrt(length))
    real = jnp.cos(theta) * scale
    imaginary = jnp.sin(theta) * (sign * scale)
    upper = jnp.stack([real, -imaginary])
    lower = jnp.stack([imaginary, real])
    return jnp.stack([upper, lower]).astype(jnp.bfloat16)


def contract(form, values, table):
    return jnp.einsum(form, values, table, preferred_element_type=jnp.float32)


def complex_product(left, right):
    return jnp.stack(
        [left[0] * right[0] - left[1] * right[1], left[0] * right[1] + left[1] * right[0]]
    )


def split_plane(plane, offset):
    cells_y, cells_x = plane.shape
    moved = pltpu.roll(plane, cells_x - offset, 1)
    bands = []
    for part in (plane + moved, plane - moved):
        bands.append((part, pltpu.roll(part, cells_y - offset, 0)))
    (low, low_moved), (high, high_moved) = bands
    return [low + low_moved, high + high_moved, low - low_moved, high - high_moved]


def merge_plane(bands, offset):
    across = []
    for lower, upper in ((bands[0], bands[2]), (bands[1], bands[3])):
        across.append(lower + upper + pltpu.roll(lower - upper, offset, 0))
    lower, upper = across
    return lower + upper + pltpu.roll(lower - upper, offset, 1)


def shrink_pair(real, imaginary, limit):
    factor = jnp.maximum(1.0 - limit * lax.rsqrt(real * real + imaginary * imaginary), 0.0)
    return real * factor, imaginary * factor


def wavelet_kernel(levels, planes, limits, source, result, *scratch):
    halo = 2**levels - 1
    stop = halo + planes
    coarse_refs = (source,) + scratch[: levels - 1]
    merged_refs = (None,) + scratch[levels - 1 : 2 * (levels - 1)]
    split_ref, carry_ref = scratch[2 * (levels - 1) :]
    extent = planes + 2 * halo
    for level in range(levels - 1):
        offset = 2**level
        extent -= offset
        finer, coarser = coarse_refs[level], coarse_refs[level + 1]

        def coarsen(n, _, offset=offset, finer=finer, coarser=coarser):
            for t in range(2):
                total = finer[t, n] + finer[t, n + offset]
                total = total + pltpu.roll(total, total.shape[1] - offset, 1)
                total = total + pltpu.roll(total, total.shape[0] - offset, 0)
                coarser[t, n] = total * half_root**3
            return 0

        lax.fori_loop(0, extent, coarsen, 0)
    for level in reversed(range(levels)):
        offset = 2**level
        slots = offset + 1
        first = halo - (offset - 1)
        start = first - offset
        coarse = coarse_refs[level]

        def enter(n, _, offset=offset, coarse=coarse, slots=slots):
            for t in range(2):
                for b, band in enumerate(split_plane(coarse[t, n] * half_root**3, offset)):
                    split_ref[lax.rem(n, slots), b, t] = band
            return 0

        lax.fori_loop(start, start + offset, enter, 0)

        def advance(n, _, level=level, offset=offset, slots=slots, first=first, enter=enter):
            enter(n + offset, 0)
            here, there, back = lax.rem(n, slots), lax.rem(n + offset, slots), lax.rem(n, offset)
            merged = [[], []]
            for b in range(4):
                near = [split_ref[here, b, t] for t in range(2)]
                far = [split_ref[there, b, t] for t in range(2)]
                high = shrink_pair(near[0] - far[0], near[1] - far[1], limits[level, b + 3])
                if b:
                    low = shrink_pair(near[0] + far[0], near[1] + far[1], limits[level, b - 1])
                elif level < levels - 1:
                    low = [merged_refs[level + 1][t, n] for t in range(2)]
                else:
                    low = (near[0] + far[0], near[1] + far[1])
                for t in range(2):
                    merged[t].append(low[t] + high[t] + carry_ref[back, b, t])
                    carry_ref[back, b, t] = low[t] - high[t]

            @pl.when(n >= first)
            def _():
                for t in range(2):
                    value = merge_plane(merged[t], offset) * quarter_root**3
                    if level:
                        merged_refs[level][t, n] = value
                    else:
                        result[t, n - halo] = value

            return 0

        lax.fori_loop(start, stop, advance, 0)


def wavelet_shrink(descent, thresholds):
    levels = thresholds.shape[0]
    halo = 2**levels - 1
    parts, planes, cells_y, cells_x = descent.shape
    ends = descent[:, planes - halo :].astype(jnp.bfloat16)
    starts = descent[:, :halo].astype(jnp.bfloat16)
    before = passed_along(ends, ("slab", "row"), 1).astype(jnp.float32)
    after = passed_along(starts, ("slab", "row"), -1).astype(jnp.float32)
    source = jnp.concatenate([before, descent, after], axis=1)
    plane = (cells_y, cells_x)
    store = [pltpu.VMEM((parts, planes + 2 * halo) + plane, jnp.float32)] * (2 * (levels - 1))
    whole = pl.BlockSpec(memory_space=pltpu.VMEM)
    return pl.pallas_call(
        functools.partial(wavelet_kernel, levels, planes),
        out_shape=jax.ShapeDtypeStruct(descent.shape, jnp.float32),
        in_specs=[pl.BlockSpec(memory_space=pltpu.SMEM), whole],
        out_specs=whole,
        scratch_shapes=store
        + [
            pltpu.VMEM((2 ** (levels - 1) + 1, 4, parts) + plane, jnp.float32),
            pltpu.VMEM((2 ** (levels - 1), 4, parts) + plane, jnp.float32),
        ],
        compiler_params=pltpu.CompilerParams(vmem_limit_bytes=32 * 2**20),
        cost_estimate=pl.CostEstimate(flops=descent.size * 400, bytes_accessed=descent.size * 8, transcendentals=0),
    )(thresholds, source)


def coil_sum(partial_value):
    total = partial_value.astype(jnp.float32)
    for distance in range(1, lax.axis_size("coil")):
        total = total + passed_along(partial_value, "coil", distance).astype(jnp.float32)
    return total


def shrinkage_step(image, sens, measured, mask, thresholds):
    shards = lax.axis_size(("slab", "row"))
    readout_cells = image.shape[3]
    phase_cells = image.shape[1]
    depth_cells = measured.shape[3]
    coils = sens.shape[1]
    table_readout = fourier_table(readout_cells, -1.0)
    inverse_readout = fourier_table(readout_cells, 1.0)
    table_phase = fourier_table(phase_cells, -1.0)
    inverse_phase = fourier_table(phase_cells, 1.0)
    table_depth = fourier_table(depth_cells, -1.0)
    inverse_depth = fourier_table(depth_cells, 1.0)
    lines = phase_cells // shards
    planes = depth_cells // shards
    phase_out = table_phase.reshape(2, 2, phase_cells, shards, lines)
    phase_in = inverse_phase.reshape(2, 2, shards, lines, phase_cells)
    depth_in = table_depth.reshape(2, 2, shards, planes, depth_cells)
    depth_out = inverse_depth.reshape(2, 2, depth_cells, shards, planes)
    sampled = mask.astype(jnp.float32)[None, None, :, :, None]
    width = max(coils // CHUNKS, 1)
    exchange = functools.partial(
        lax.all_to_all, axis_name=("slab", "row"), split_axis=0, concat_axis=0, tiled=True
    )
    gradient = jnp.zeros((2, phase_cells, planes, readout_cells), jnp.float32)
    previous = None
    for first in range(0, coils, width):
        part = slice(first, first + width)
        sens_part, image_part = sens[:, part], image
        if previous is not None:
            sens_part, image_part, _ = lax.optimization_barrier((sens_part, image, previous))
        sens_wide = sens_part.astype(jnp.float32)
        coil_image = complex_product(sens_wide, image_part[:, None]).astype(jnp.bfloat16)
        readout_done = contract("tcyzj,stjk->scyzk", coil_image, table_readout).astype(jnp.bfloat16)
        phase_done = contract("tcjzx,stjdk->dsckzx", readout_done, phase_out).astype(jnp.bfloat16)
        previous = phase_done
        spread = exchange(phase_done)
        spectrum = contract("dtcyjx,stdjk->scykx", spread, depth_in)
        residual = (sampled * (spectrum - measured[:, part].astype(jnp.float32))).astype(jnp.bfloat16)
        depth_back = contract("tcyjx,stjdk->dscykx", residual, depth_out).astype(jnp.bfloat16)
        gathered = exchange(depth_back)
        phase_back = contract("dtcjzx,stdjk->sckzx", gathered, phase_in).astype(jnp.bfloat16)
        readout_back = contract("tcyzj,stjk->scyzk", phase_back, inverse_readout)
        gradient = gradient + jnp.stack(
            [
                jnp.sum(sens_wide[0] * readout_back[0] + sens_wide[1] * readout_back[1], axis=0),
                jnp.sum(sens_wide[0] * readout_back[1] - sens_wide[1] * readout_back[0], axis=0),
            ]
        )
    turned = jnp.swapaxes(gradient.astype(jnp.bfloat16), 1, 2)
    descent = jnp.swapaxes(image, 1, 2) - step_size * coil_sum(turned)
    return jnp.swapaxes(wavelet_shrink(descent, thresholds), 1, 2)


def solution(mesh):
    return jax.shard_map(
        shrinkage_step,
        mesh=mesh,
        in_specs=(
            P("groups", None, ("slab", "row"), None),
            P("groups", "coil", None, ("slab", "row"), None),
            P("groups", "coil", ("slab", "row"), None, None),
            P(("slab", "row"), None),
            P(),
        ),
        out_specs=P("groups", None, ("slab", "row"), None),
        check_vma=False,
    )
```

time: 731 us -> 488 us (0.67)
  blocking collectives: 219 us -> 0 us
  other arithmetic: 166 us -> 27.4 us
  waiting for transfers between devices: 188 us -> 282 us
  starting transfers between devices: 16 us -> 85.4 us
  local copies, waits for them, and re-layouts: 86.6 us -> 30.6 us
  Pallas kernels: 0 us -> 21.7 us
  between operations: 14.1 us -> 0.34 us
    all_to_all x1 -> x0, blocking collectives: 219 us -> none  [local(): lax.all_to_all(depth_back, ('slab', 'row'), split_axis=3, concat_axis=2,...]
    all_to_all x1 -> x4, waiting for transfers between devices: 147 us -> 254 us  [the longest x2 128 us: shrinkage_step(): gathered = exchange(depth_back)]
    mul x15 -> x2, other arithmetic: 88.5 us -> 0.01 us  [fourier_table(): phase = index[:, None] * index[None, :] % length]
    all_to_all x1 -> x4, starting transfers between devices: 7.6 us -> 66.6 us  [the longest x2 39.4 us: shrinkage_step(): gathered = exchange(depth_back)]
    psum x1 -> x0, waiting for transfers between devices: 39.3 us -> none  [local(): lax.psum(partial_value.astype(jnp.bfloat16), 'coil').astype(jnp.float32)]
    ppermute x4 -> x3, waiting for transfers between devices: 1.23 us -> 27.7 us  [passed_along(): return lax.ppermute(block, axis, route)]
    all_to_all x2 -> x0, local copies, waits for them, and re-layouts: 25.5 us -> none  [the longest x1 16.3 us: local(): lax.all_to_all(depth_back, ('slab', 'row'), split_axis=3, concat_axis=2,...]
    pallas_call x0 -> x1, Pallas kernels: none -> 21.7 us  [wavelet_shrink(): pl.pallas_call(functools.partial(wavelet_kernel, levels, planes), out_sha...]
  transfers between devices with their start and end apart: 6 -> 7, of which waited for: 4 -> 7; matrix products, arithmetic and copies ran while one was open for 6% -> 11% of each run, Pallas kernels for 0% -> 0%
where the time goes in v1:
time: 488 us; the launch traced here: 487 us
  waiting for transfers between devices  282 us (58%)
  starting transfers between devices  85.4 us (18%)
  matrix products  40.2 us (8%)
  local copies, waits for them, and re-layouts  30.6 us (6%)
  other arithmetic  27.4 us (6%)
  Pallas kernels  21.7 us (4%)
    all_to_all x2, waiting for transfers between devices, shrinkage_step(): gathered = exchange(depth_back)  128 us
    all_to_all x2, waiting for transfers between devices, shrinkage_step(): spread = exchange(phase_done)  127 us
    dot_general x9, matrix products, contract(): return jnp.einsum(form, values, table, preferred_element_type=jnp.float32)  40.2 us
    all_to_all x2, starting transfers between devices, shrinkage_step(): gathered = exchange(depth_back)  39.4 us
    ppermute x3, waiting for transfers between devices, passed_along(): return lax.ppermute(block, axis, route)  27.7 us
    all_to_all x2, starting transfers between devices, shrinkage_step(): spread = exchange(phase_done)  27.2 us
    pallas_call x1, Pallas kernels, wavelet_shrink(): pl.pallas_call(functools.partial(wavelet_kernel, levels, planes), out_sha...  21.7 us
    ppermute x3, starting transfers between devices, passed_along(): return lax.ppermute(block, axis, route)  18.8 us
  transfers between devices with their start and end apart: 7, of which 7 were waited for; matrix products, arithmetic and copies ran while one was open for 11% of the time, Pallas kernels for 0%

profile of v1, /device:TPU:0, one launch (start us, length us, event | category | flops | bytes accessed | tf_op | source)
XLA Modules:
  0.0 487.4 jit_solution(1533827634891933236)
XLA Ops:
  13.0 5.2 %fusion.7 = bf16[16,2,4,8,16,128]{5,3,4,2,0,1:T(8,128)(2,1)} fusion(bf16[1,4,128,16,128]{4,2,0,3,1:T(8,128)(2,1)} %get-tuple-element.18, bf16[1,4,128,16,128]{4,2,0,3,1:T(8,128)(2,1)S(1)} %get-tuple-element.17, bf16[1,2,128,128]{2,3,1,0:T(8,128)(2,1)S(1)} %get-tuple-element.28, bf16[1,2,128,128]{2,3,1,0:T(8,128)(2,1)S(1)} %get-tuple-element.29, ...), kind=kOutput, calls=%fused_computation.16 | convolution fusion | flops 2160852992 | bytes 8617984 | tf_op jit(solution)/shard_map/tcjzx,stjdk->dsckzx/dot_general | solution.py:36
  18.2 4.8 copy.32
  23.0 7.5 %all-to-all-start = ((bf16[16,2,4,8,16,128]{5,3,4,2,1,0:T(8,128)(2,1)}), bf16[16,2,4,8,16,128]{5,3,4,2,1,0:T(8,128)(2,1)}, u32[]{:S(2)}, u32[]{:S(2)}) async-start(bf16[16,2,4,8,16,128]{5,3,4,2,1,0:T(8,128)(2,1)} %copy.32), calls=%async_computation | async-start | bytes 8388608 | tf_op jit(solution)/shard_map/all_to_all | solution.py:205
  30.5 3.4 copy.110
  41.7 3.2 copy.47
  44.9 63.1 %all-to-all-done = bf16[16,2,4,8,16,128]{5,3,4,2,1,0:T(8,128)(2,1)} async-done(((bf16[16,2,4,8,16,128]{5,3,4,2,1,0:T(8,128)(2,1)}), bf16[16,2,4,8,16,128]{5,3,4,2,1,0:T(8,128)(2,1)}, u32[]{:S(2)}, u32[]{:S(2)}) %all-to-all-start) | async-done | bytes 4194336 | tf_op jit(solution)/shard_map/all_to_all | solution.py:205
  108.0 19.7 %all-to-all-start.2 = ((bf16[16,2,4,8,16,128]{5,4,2,3,1,0:T(8,128)(2,1)}), bf16[16,2,4,8,16,128]{5,4,2,3,1,0:T(8,128)(2,1)}, u32[]{:S(2)}, u32[]{:S(2)}) async-start(bf16[16,2,4,8,16,128]{5,4,2,3,1,0:T(8,128)(2,1)} %copy.47), calls=%async_computation.2 | async-start | bytes 8388608 | tf_op jit(solution)/shard_map/all_to_all | solution.py:205
  130.3 6.1 %fusion.13 = bf16[2,4,8,256,128,1,1]{4,3,2,1,0,6,5:T(8,128)(2,1)S(1)} fusion(bf16[2,8,8,256,128]{4,3,2,1,0:T(8,128)(2,1)} %param.7, f32[8,256]{1,0:T(8,128)S(1)} %convert_element_type.238, bf16[16,2,4,8,16,128]{5,3,4,2,1,0:T(8,128)(2,1)} %all-to-all-done, bf16[1,1,16,16,256]{4,3,1,2,0:T(8,128)(2,1)S(1)} %get-tuple-element.39, ...), kind=kOutput, calls=%fused_computation.21 | convolution fusion | flops 2157969408 | bytes 12984320 | tf_op jit(solution)/shard_map/dtcyjx,stdjk->scykx/dot_general | solution.py:36
  138.8 3.0 copy.36
  141.8 63.4 %all-to-all-done.2 = bf16[16,2,4,8,16,128]{5,4,2,3,1,0:T(8,128)(2,1)} async-done(((bf16[16,2,4,8,16,128]{5,4,2,3,1,0:T(8,128)(2,1)}), bf16[16,2,4,8,16,128]{5,4,2,3,1,0:T(8,128)(2,1)}, u32[]{:S(2)}, u32[]{:S(2)}) %all-to-all-start.2) | async-done | bytes 4194336 | tf_op jit(solution)/shard_map/all_to_all | solution.py:205
  205.3 19.7 %all-to-all-start.1 = ((bf16[16,2,4,8,16,128]{5,3,2,4,1,0:T(8,128)(2,1)}), bf16[16,2,4,8,16,128]{5,3,2,4,1,0:T(8,128)(2,1)}, u32[]{:S(2)}, u32[]{:S(2)}) async-start(bf16[16,2,4,8,16,128]{5,3,2,4,1,0:T(8,128)(2,1)} %copy.36), calls=%async_computation.1 | async-start | bytes 8388608 | tf_op jit(solution)/shard_map/all_to_all | solution.py:209
  225.0 5.8 %fusion.17 = bf16[2,4,8,256,128,1,1]{4,3,2,1,0,6,5:T(8,128)(2,1)S(1)} fusion(bf16[2,8,8,256,128]{4,3,2,1,0:T(8,128)(2,1)} %param.7, f32[8,256]{1,0:T(8,128)S(1)} %convert_element_type.238, bf16[16,2,4,8,16,128]{5,4,2,3,1,0:T(8,128)(2,1)} %all-to-all-done.2, bf16[1,1,16,16,256]{4,3,1,2,0:T(8,128)(2,1)S(1)} %get-tuple-element.39, ...), kind=kOutput, calls=%fused_computation.24 | convolution fusion | flops 2157969408 | bytes 12984320 | tf_op jit(solution)/shard_map/dtcyjx,stdjk->scykx/dot_general | solution.py:36
  233.2 3.0 copy.51
  236.2 66.3 %all-to-all-done.1 = bf16[16,2,4,8,16,128]{5,3,2,4,1,0:T(8,128)(2,1)} async-done(((bf16[16,2,4,8,16,128]{5,3,2,4,1,0:T(8,128)(2,1)}), bf16[16,2,4,8,16,128]{5,3,2,4,1,0:T(8,128)(2,1)}, u32[]{:S(2)}, u32[]{:S(2)}) %all-to-all-start.1) | async-done | bytes 4194336 | tf_op jit(solution)/shard_map/all_to_all | solution.py:209
  302.5 19.7 %all-to-all-start.3 = ((bf16[16,2,4,8,16,128]{5,3,2,4,1,0:T(8,128)(2,1)}), bf16[16,2,4,8,16,128]{5,3,2,4,1,0:T(8,128)(2,1)}, u32[]{:S(2)}, u32[]{:S(2)}) async-start(bf16[16,2,4,8,16,128]{5,3,2,4,1,0:T(8,128)(2,1)} %copy.51), calls=%async_computation.3 | async-start | bytes 8388608 | tf_op jit(solution)/shard_map/all_to_all | solution.py:209
  322.6 7.9 %fusion.45 = f32[2,4,128,16,128]{4,2,0,3,1:T(8,128)} fusion(bf16[1,1,16,8,128]{4,3,1,2,0:T(8,128)(2,1)S(1)} %get-tuple-element.33, bf16[1,1,16,8,128]{4,3,1,2,0:T(8,128)(2,1)S(1)} %get-tuple-element.32, bf16[1,1,16,8,128]{4,3,1,2,0:T(8,128)(2,1)S(1)} %get-tuple-element.31, bf16[1,2,128,128]{2,3,1,0:T(8,128)(2,1)S(1)} %get-tuple-element.30, ...), kind=kOutput, calls=%fused_computation.60 | convolution fusion | flops 2150367232 | bytes 12812288 | tf_op jit(solution)/shard_map/tcyzj,stjk->scyzk/dot_general | solution.py:36
  330.4 8.1 %add_reduce_fusion.1 = (f32[128,16,128]{2,0,1:T(8,128)S(1)}, f32[128,16,128]{2,0,1:T(8,128)}) fusion(f32[2,4,128,16,128]{4,2,0,3,1:T(8,128)} %fusion.45, f32[2,4,128,16,128]{4,2,0,3,1:T(8,128)} %copy-done.1), kind=kLoop, calls=%fused_computation.56 | loop fusion | flops 7864320 | bytes 18874368 | tf_op jit(solution)/shard_map/reduce_sum | solution.py:214
  338.5 61.2 %all-to-all-done.3 = bf16[16,2,4,8,16,128]{5,3,2,4,1,0:T(8,128)(2,1)} async-done(((bf16[16,2,4,8,16,128]{5,3,2,4,1,0:T(8,128)(2,1)}), bf16[16,2,4,8,16,128]{5,3,2,4,1,0:T(8,128)(2,1)}, u32[]{:S(2)}, u32[]{:S(2)}) %all-to-all-start.3) | async-done | bytes 4194336 | tf_op jit(solution)/shard_map/all_to_all | solution.py:209
  399.8 7.9 %fusion.42 = f32[2,4,128,16,128]{4,2,0,3,1:T(8,128)} fusion(bf16[1,1,16,8,128]{4,3,1,2,0:T(8,128)(2,1)S(1)} %get-tuple-element.33, bf16[1,1,16,8,128]{4,3,1,2,0:T(8,128)(2,1)S(1)} %get-tuple-element.32, bf16[1,1,16,8,128]{4,3,1,2,0:T(8,128)(2,1)S(1)} %get-tuple-element.31, bf16[1,2,128,128]{2,3,1,0:T(8,128)(2,1)S(1)} %get-tuple-element.30, ...), kind=kOutput, calls=%fused_computation.59 | convolution fusion | flops 2150367232 | bytes 12812288 | tf_op jit(solution)/shard_map/tcyzj,stjk->scyzk/dot_general | solution.py:36
  407.6 7.2 %add_reduce_fusion = (f32[128,16,128]{2,0,1:T(8,128)S(1)}, f32[128,16,128]{2,0,1:T(8,128)S(1)}) fusion(f32[2,4,128,16,128]{4,2,0,3,1:T(8,128)} %fusion.42, f32[2,4,128,16,128]{4,2,0,3,1:T(8,128)} %copy-done.2), kind=kLoop, calls=%fused_computation.52 | loop fusion | flops 7864320 | bytes 18874368 | tf_op jit(solution)/shard_map/reduce_sum | solution.py:214
  416.7 24.5 %collective-permute-done = bf16[2,16,128,128]{3,2,1,0:T(8,128)(2,1)S(1)} collective-permute-done((bf16[2,16,128,128]{3,2,1,0:T(8,128)(2,1)S(1)}, bf16[2,16,128,128]{3,2,1,0:T(8,128)(2,1)S(1)}, u32[]{:S(2)}, u32[]{:S(2)}) %collective-permute-start) | collective-permute-done | bytes 1048608 | tf_op jit(solution)/shard_map/ppermute | solution.py:20
  442.5 17.1 %collective-permute-start.2 = (bf16[2,3,128,128]{3,2,1,0:T(8,128)(2,1)S(1)}, bf16[2,3,128,128]{3,2,1,0:T(8,128)(2,1)S(1)}, u32[]{:S(2)}, u32[]{:S(2)}) collective-permute-start(bf16[2,3,128,128]{3,2,1,0:T(8,128)(2,1)S(1)} %get-tuple-element.26), channel_id=1, source_target_pairs={{1,0},{4,1},{5,4},{8,5},{9,8},{12,9},{13,12},{16,13},{17,16},{20,1... | collective-permute-start | bytes 589832 | tf_op jit(solution)/shard_map/ppermute | solution.py:20
  459.6 3.0 collective-permute-done.1
  463.2 21.7 %shard_map.55 = f32[2,16,128,128]{3,2,1,0:T(8,128)S(1)} custom-call(f32[2,7]{1,0:T(2,128)S(1)} %copy-done, f32[2,22,128,128]{3,2,1,0:T(8,128)S(1)} %pad_maximum_fusion.source), custom_call_target="tpu_custom_call" | custom-call | flops 209715200 | bytes 4194304 | tf_op jit(solution)/shard_map/pallas_call | solution.py:148
  (50 shorter events, 34.5 us)
Async XLA Ops:
  1.2 4.0 copy-start.5
  9.1 3.9 copy-start.1
  23.0 85.0 %all-to-all-start = ((bf16[16,2,4,8,16,128]{5,3,4,2,1,0:T(8,128)(2,1)}), bf16[16,2,4,8,16,128]{5,3,4,2,1,0:T(8,128)(2,1)}, u32[]{:S(2)}, u32[]{:S(2)}) async-start(bf16[16,2,4,8,16,128]{5,3,4,2,1,0:T(8,128)(2,1)} %copy.32), calls=%async_computation | async-start | bytes 8388608 | tf_op jit(solution)/shard_map/all_to_all | solution.py:205
  30.5 3.5 copy-start.3
  35.9 3.2 copy-start.2
  44.9 82.9 %copy-start.6 = (s32[8,256]{1,0:T(8,128)S(1)}, s32[8,256]{1,0:T(8,128)}, u32[]{:S(2)}) copy-start(s32[8,256]{1,0:T(8,128)} %param.8) | copy-start | bytes 24580
  108.0 97.2 %all-to-all-start.2 = ((bf16[16,2,4,8,16,128]{5,4,2,3,1,0:T(8,128)(2,1)}), bf16[16,2,4,8,16,128]{5,4,2,3,1,0:T(8,128)(2,1)}, u32[]{:S(2)}, u32[]{:S(2)}) async-start(bf16[16,2,4,8,16,128]{5,4,2,3,1,0:T(8,128)(2,1)} %copy.47), calls=%async_computation.2 | async-start | bytes 8388608 | tf_op jit(solution)/shard_map/all_to_all | solution.py:205
  205.3 97.2 %all-to-all-start.1 = ((bf16[16,2,4,8,16,128]{5,3,2,4,1,0:T(8,128)(2,1)}), bf16[16,2,4,8,16,128]{5,3,2,4,1,0:T(8,128)(2,1)}, u32[]{:S(2)}, u32[]{:S(2)}) async-start(bf16[16,2,4,8,16,128]{5,3,2,4,1,0:T(8,128)(2,1)} %copy.36), calls=%async_computation.1 | async-start | bytes 8388608 | tf_op jit(solution)/shard_map/all_to_all | solution.py:209
  302.5 97.2 %all-to-all-start.3 = ((bf16[16,2,4,8,16,128]{5,3,2,4,1,0:T(8,128)(2,1)}), bf16[16,2,4,8,16,128]{5,3,2,4,1,0:T(8,128)(2,1)}, u32[]{:S(2)}, u32[]{:S(2)}) async-start(bf16[16,2,4,8,16,128]{5,3,2,4,1,0:T(8,128)(2,1)} %copy.51), calls=%async_computation.3 | async-start | bytes 8388608 | tf_op jit(solution)/shard_map/all_to_all | solution.py:209
  407.6 7.2 %copy-start.4 = (f32[128,16,128]{2,0,1:T(8,128)S(1)}, f32[128,16,128]{2,0,1:T(8,128)}, u32[]{:S(2)}) copy-start(f32[128,16,128]{2,0,1:T(8,128)} %get-tuple-element.10) | copy-start | bytes 3145732
  415.1 26.1 %collective-permute-start = (bf16[2,16,128,128]{3,2,1,0:T(8,128)(2,1)S(1)}, bf16[2,16,128,128]{3,2,1,0:T(8,128)(2,1)S(1)}, u32[]{:S(2)}, u32[]{:S(2)}) collective-permute-start(bf16[2,16,128,128]{3,2,1,0:T(8,128)(2,1)S(1)} %fusion.69), channel_id=1, source_target_pairs={{2,0},{0,2},{3,1},{1,3},{6,4},{4,6},{7,5},{5,7},{10,8},{8,10},{11,... | collective-permute-start | bytes 3145736 | tf_op jit(solution)/shard_map/ppermute | solution.py:20
  442.3 20.8 %copy-start = (f32[2,7]{1,0:T(2,128)S(1)}, f32[2,7]{1,0:T(2,128)}, u32[]{:S(2)}) copy-start(f32[2,7]{1,0:T(2,128)} %limits.1) | copy-start | bytes 172
  442.3 20.2 %collective-permute-start.1 = (bf16[2,3,128,128]{3,2,1,0:T(8,128)(2,1)S(1)}, bf16[2,3,128,128]{3,2,1,0:T(8,128)(2,1)S(1)}, u32[]{:S(2)}, u32[]{:S(2)}) collective-permute-start(bf16[2,3,128,128]{3,2,1,0:T(8,128)(2,1)S(1)} %get-tuple-element.25), channel_id=1, source_target_pairs={{29,0},{0,1},{1,4},{4,5},{5,8},{8,9},{9,12},{12,13},{13,16},{16,17... | collective-permute-start | bytes 589832 | tf_op jit(solution)/shard_map/ppermute | solution.py:20
  442.5 20.3 %collective-permute-start.2 = (bf16[2,3,128,128]{3,2,1,0:T(8,128)(2,1)S(1)}, bf16[2,3,128,128]{3,2,1,0:T(8,128)(2,1)S(1)}, u32[]{:S(2)}, u32[]{:S(2)}) collective-permute-start(bf16[2,3,128,128]{3,2,1,0:T(8,128)(2,1)S(1)} %get-tuple-element.26), channel_id=1, source_target_pairs={{1,0},{4,1},{5,4},{8,5},{9,8},{12,9},{13,12},{16,13},{17,16},{20,1... | collective-permute-start | bytes 589832 | tf_op jit(solution)/shard_map/ppermute | solution.py:20
